TPU v7x, 32 devices: a whole 2x2x4 slice. The times are simulated.
32 devices in a mesh: grp: 8 (over y, x, core), rep: 4 (over z).
Axes of the slice: x: 2, y: 2, z: 4, core: 2. Of those that a mesh axis runs over, the one named last changes fastest.
Arguments:
- momentum: bfloat16 [256, 4096], P(('grp', 'rep')), may hold values from -6 to 6
- picked: int32 [256, 32], P(('grp', 'rep')), may hold values from 0 to 4095, as said below
- owner_span_order: int32 [8], replicated, may hold values from 0 to 7, each once
Outputs:
- update: bfloat16 [8, 4096], replicated
- residual_momentum: bfloat16 [256, 4096], P(('grp', 'rep'))
Inputs may be any that keep to these rules, and one draw needn't show every extreme that they name: `picked`: the 32 numbers of a row are different. `owner_span_order`: each span stands once.
All inputs are finite; a program needn't handle non-finite values.
Results may differ from a plain program's by a relative error of at most 0.013.
Values may be sent and summed in bfloat16 or wider, within the bound.
A program may use at most 64 MiB of HBM per device.

v0:
```python
import math
import jax
import jax.numpy as jnp
from jax import lax
from jax.sharding import PartitionSpec as P

BLOCK = 64
TOPK = 32
CH_OWN = 1


def dct_cosines(points):
    freq = jnp.arange(points, dtype=jnp.float32)[:, None]
    place = jnp.arange(points, dtype=jnp.float32)[None, :]
    values = jnp.cos(jnp.pi * (2.0 * place + 1.0) * freq / (2.0 * points)) * jnp.sqrt(2.0 / points)
    values = values.at[0].multiply(jnp.sqrt(0.5))
    rounded = lax.optimization_barrier(values.astype(jnp.bfloat16))
    return rounded.astype(jnp.float32)


def forward(square_low, cosines, cos_low):
    half = jnp.einsum("cab,jb->caj", square_low, cos_low, preferred_element_type=jnp.float32)
    return jnp.einsum("ia,caj->cij", cosines, half, precision=lax.Precision.HIGHEST)


def decode(dense_matrix, cosines):
    square = dense_matrix.reshape(dense_matrix.shape[0], BLOCK, BLOCK)
    half = jnp.einsum("cij,jb->cib", square, cosines, precision=lax.Precision.HIGHEST)
    full = jnp.einsum("ia,cib->cab", cosines, half, precision=lax.Precision.HIGHEST)
    return full.reshape(dense_matrix.shape[0], BLOCK * BLOCK)


def decode_sparse(dense_low, cosines, cos_low):
    square = dense_low.reshape(dense_low.shape[0], BLOCK, BLOCK)
    half = jnp.einsum("cij,jb->cib", square, cos_low, preferred_element_type=jnp.float32)
    full = jnp.einsum("ia,cib->cab", cosines, half, precision=lax.Precision.HIGHEST)
    return full.reshape(dense_low.shape[0], BLOCK * BLOCK)


def densify(values, spots):
    entries, columns = values.shape
    per_step = math.gcd(entries, max(1, 65536 // columns))
    positions = jnp.arange(BLOCK, dtype=jnp.int32)

    def one_block(pieces):
        block_values, block_spots = pieces
        zeros = jnp.zeros_like(block_values)
        row_onehot = jnp.where(
            (block_spots // BLOCK)[:, None, :] == positions[None, :, None],
            block_values[:, None, :],
            zeros[:, None, :],
        )
        column_onehot = ((block_spots % BLOCK)[:, None, :] == positions[None, :, None]).astype(
            jnp.bfloat16
        )
        dense_matrix = jnp.einsum(
            "bcy,bzy->bcz", row_onehot, column_onehot, preferred_element_type=jnp.float32
        )
        return dense_matrix.reshape(per_step, BLOCK * BLOCK)

    stacked = lax.map(
        one_block,
        (
            values.reshape(entries // per_step, per_step, columns),
            spots.reshape(entries // per_step, per_step, columns),
        ),
    )
    return stacked.reshape(entries, BLOCK * BLOCK)


def owner_sum(received):
    values, spots = received
    return densify(values[0], spots[0])


def local(momentum, picked, owner_span_order):
    cosines = dct_cosines(BLOCK)
    cos_low = cosines.astype(jnp.bfloat16)
    owners = lax.axis_size("grp")
    span_count = momentum.shape[0]
    square_low = momentum.reshape(span_count, BLOCK, BLOCK)
    transform_coefficients = forward(square_low, cosines, cos_low).reshape(
        span_count, BLOCK * BLOCK
    )
    chosen = jnp.take_along_axis(transform_coefficients, picked, axis=1).astype(jnp.bfloat16)
    own_dense = densify(chosen, picked).astype(jnp.bfloat16)
    residual_momentum = (
        momentum.astype(jnp.float32) - decode_sparse(own_dense, cosines, cos_low)
    ).astype(jnp.bfloat16)
    slot_values = jnp.take(chosen, owner_span_order, axis=0)
    slot_spots = jnp.take(picked, owner_span_order, axis=0)
    shaped = (slot_values.reshape(owners, CH_OWN, TOPK), slot_spots.reshape(owners, CH_OWN, TOPK))
    partial_sum = owner_sum(
        (
            lax.all_to_all(shaped[0], "grp", split_axis=0, concat_axis=2, tiled=True),
            lax.all_to_all(shaped[1], "grp", split_axis=0, concat_axis=2, tiled=True),
        )
    )
    partial_sum = lax.psum(partial_sum, "rep")
    my_share = decode(partial_sum, cosines).astype(jnp.bfloat16)
    update = lax.all_gather(my_share, "grp", axis=0, tiled=True)
    return (update, residual_momentum)


def solution(mesh):
    return jax.shard_map(
        local,
        mesh=mesh,
        in_specs=(P(("grp", "rep"), None), P(("grp", "rep"), None), P()),
        out_specs=(P(), P(("grp", "rep"), None)),
        check_vma=False,
    )
```

profile of v0, /device:TPU:0, one launch (start us, length us, event | category | flops | bytes accessed | tf_op | source)
XLA Modules:
  0.0 55.1 jit_solution(13529057157685993092)
XLA Ops:
  0.6 0.7 %compare_and_fusion = pred[8]{0:T(512)(128)(4,1)S(1)} fusion(s32[8]{0:T(128)} %param.7), kind=kLoop, calls=%fused_computation.49 | loop fusion | flops 48 | bytes 40 | tf_op jit(solution)/shard_map/jit(_take)/and | solution.py:90
  1.4 0.6 %copy-done = s32[8,32]{1,0:T(8,128)S(1)} copy-done((s32[8,32]{1,0:T(8,128)S(1)}, s32[8,32]{1,0:T(8,128)}, u32[]{:S(2)}) %copy-start) | copy-done | bytes 1048
  2.1 0.1 cosine_multiply_fusion
  2.4 0.2 reshape.317
  2.5 0.3 convolution_bitcast_fusion.2
  2.8 0.3 convolution_bitcast_fusion.1
  3.1 0.1 copy.19
  3.2 0.2 reshape.318
  3.4 2.4 %gather_fusion.2 = bf16[256]{0:T(256)(128)(2,1)S(1)} fusion(bf16[8,4096]{1,0:T(8,128)(2,1)S(1)} %reshape.318, s32[256]{0:T(256)S(1)} %reshape.340), kind=kCustom, calls=%fused_computation.2 | custom fusion | bytes 3072 | tf_op jit(solution)/shard_map/jit(take_along_axis)/gather | solution.py:85
  5.9 0.6 %gather_fusion.1 = bf16[8,32]{1,0:T(8,128)(2,1)S(1)} fusion(bf16[8,32]{1,0:T(8,128)(2,1)S(1)} %select_convert_fusion, s32[1024]{0:T(1024)S(1)} %pad_clamp_fusion), kind=kCustom, calls=%fused_computation.1 | custom fusion | bytes 1056 | tf_op jit(solution)/shard_map/jit(_take)/gather | solution.py:90
  6.5 0.6 %copy.20 = bf16[8,1,32]{2,1,0:T(2,128)(2,1)} copy(bf16[8,1,32]{2,0,1:T(8,128)(2,1)S(1)} %bitcast_select_fusion.1) | data formatting | bytes 1024 | tf_op jit(solution)/shard_map/jit(_take)/select_n | solution.py:90
  7.1 5.2 %all-to-all-start.1 = ((bf16[8,1,32]{2,1,0:T(2,128)(2,1)}), bf16[8,1,32]{2,1,0:T(2,128)(2,1)S(1)}, u32[]{:S(2)}, u32[]{:S(2)}) async-start(bf16[8,1,32]{2,1,0:T(2,128)(2,1)} %copy.20), calls=%async_computation.1 | async-start | bytes 8192 | tf_op jit(solution)/shard_map/all_to_all | solution.py:95
  12.3 0.6 %gather_fusion = s32[8,32]{1,0:T(8,128)S(1)} fusion(s32[8,32]{1,0:T(8,128)S(1)} %copy-done, s32[1024]{0:T(1024)S(1)} %pad_clamp_fusion), kind=kCustom, calls=%fused_computation | custom fusion | bytes 2080 | tf_op jit(solution)/shard_map/jit(_take)/gather | solution.py:91
  12.9 0.6 %fusion = f32[8,64,64]{1,2,0:T(8,128)S(1)} fusion(s32[8,32]{1,0:T(8,128)S(1)} %get-tuple-element.45, s32[8,32]{1,0:T(8,128)S(1)} %get-tuple-element.44, bf16[8,32]{1,0:T(8,128)(2,1)S(1)} %select_convert_fusion, bf16[64,64]{1,0:T(8,128)(2,1)S(1)} %convert_element_type.42), kind=kOutput, calls=%fused_computation.7 | convolution fusion | flops 6373376 | bytes 141824 | tf_op jit(solution)/shard_map/cij,jb->cib/dot_general | solution.py:35
  13.5 0.3 convolution_bitcast_fusion
  13.8 0.7 %bitcast_select_fusion = s32[8,1,32]{2,0,1:T(8,128)} fusion(s32[8,32]{1,0:T(8,128)S(1)} %gather_fusion, pred[8]{0:T(512)(128)(4,1)S(1)} %compare_and_fusion), kind=kLoop, calls=%fused_computation.40 | loop fusion | flops 256 | bytes 2056 | tf_op jit(solution)/shard_map/jit(_take)/select_n | solution.py:91
  14.4 0.1 copy.23
  14.6 0.1 reshape.322
  14.7 2.3 %all-to-all-done.1 = bf16[8,1,32]{2,1,0:T(2,128)(2,1)S(1)} async-done(((bf16[8,1,32]{2,1,0:T(2,128)(2,1)}), bf16[8,1,32]{2,1,0:T(2,128)(2,1)S(1)}, u32[]{:S(2)}, u32[]{:S(2)}) %all-to-all-start.1) | async-done | bytes 544 | tf_op jit(solution)/shard_map/all_to_all | solution.py:95
  16.9 3.3 %all-to-all-start = ((s32[8,1,32]{2,1,0:T(1,128)}), s32[8,1,32]{2,1,0:T(1,128)S(1)}, u32[]{:S(2)}, u32[]{:S(2)}) async-start(s32[8,1,32]{2,1,0:T(1,128)} %bitcast.1), calls=%async_computation | async-start | bytes 8192 | tf_op jit(solution)/shard_map/all_to_all | solution.py:96
  20.3 0.6 %subtract_convert_fusion = bf16[8,4096]{1,0:T(8,128)(2,1)} fusion(f32[8,4096]{1,0:T(8,128)S(1)} %reshape.322, bf16[8,4096]{1,0:T(8,128)(2,1)S(1)} %copy-done.1), kind=kLoop, calls=%fused_computation.10 | loop fusion | flops 98304 | bytes 262144 | tf_op jit(solution)/shard_map/convert_element_type | solution.py:89
  21.0 3.8 %all-to-all-done = s32[8,1,32]{2,1,0:T(1,128)S(1)} async-done(((s32[8,1,32]{2,1,0:T(1,128)}), s32[8,1,32]{2,1,0:T(1,128)S(1)}, u32[]{:S(2)}, u32[]{:S(2)}) %all-to-all-start) | async-done | bytes 1056 | tf_op jit(solution)/shard_map/all_to_all | solution.py:96
  24.8 0.5 broadcast.298
  25.3 0.7 %reduce.6 = s32[8,32]{1,0:T(8,128)S(1)} reduce(s32[8,1,32]{2,1,0:T(1,128)S(1)} %all-to-all-done, s32[]{:T(128)} %broadcast.298), dimensions={1}, to_apply=%all_to_all.4.reduce_sub_computation.3 | reduce | bytes 2052 | tf_op jit(solution)/shard_map/all_to_all | solution.py:96
  26.1 0.1 fusion.10
  26.2 19.4 %psum.7 = f32[64,64]{1,0:T(8,128)S(1)} all-reduce(f32[64,64]{1,0:T(8,128)S(1)} %fusion.10), channel_id=1, replica_groups=mesh['grp'=8,'rep'=4] {'rep'}, use_global_device_ids=true, to_apply=%region_0.0 | all-reduce | flops 4096 | bytes 32768 | tf_op jit(solution)/shard_map/psum | solution.py:99
  45.6 0.1 fusion.29
  45.7 0.2 fusion.1
  46.0 0.1 copy.21
  46.1 0.1 reshape.353
  46.2 8.3 %all-gather = bf16[8,1,4096]{2,1,0:T(2,128)(2,1)S(1)} all-gather(bf16[1,1,4096]{2,1,0:T(2,128)(2,1)S(1)} %reshape.353), channel_id=1, replica_groups=mesh['grp'=8,'rep'=4] {'grp'}, dimensions={0}, use_global_device_ids=true | all-gather | bytes 73728 | tf_op jit(solution)/shard_map/all_gather | solution.py:101
  54.4 0.7 %copy.27 = bf16[8,1,4096]{2,0,1:T(8,128)(2,1)} copy(bf16[8,1,4096]{2,1,0:T(2,128)(2,1)S(1)} %all-gather) | data formatting | bytes 131072
  (21 shorter events, 0.5 us)
Async XLA Ops:
  0.6 0.7 %copy-start.2 = (s32[8]{0:T(128)S(1)}, s32[8]{0:T(128)}, u32[]{:S(2)}) copy-start(s32[8]{0:T(128)} %param.7) | copy-start | bytes 100
  1.4 0.7 %copy-start = (s32[8,32]{1,0:T(8,128)S(1)}, s32[8,32]{1,0:T(8,128)}, u32[]{:S(2)}) copy-start(s32[8,32]{1,0:T(8,128)} %param.6) | copy-start | bytes 3076
  1.4 1.0 %copy-start.1 = (bf16[8,4096]{1,0:T(8,128)(2,1)S(1)}, bf16[8,4096]{1,0:T(8,128)(2,1)}, u32[]{:S(2)}) copy-start(bf16[8,4096]{1,0:T(8,128)(2,1)} %param.5) | copy-start | bytes 196612
  7.1 9.8 %all-to-all-start.1 = ((bf16[8,1,32]{2,1,0:T(2,128)(2,1)}), bf16[8,1,32]{2,1,0:T(2,128)(2,1)S(1)}, u32[]{:S(2)}, u32[]{:S(2)}) async-start(bf16[8,1,32]{2,1,0:T(2,128)(2,1)} %copy.20), calls=%async_computation.1 | async-start | bytes 8192 | tf_op jit(solution)/shard_map/all_to_all | solution.py:95
  16.9 7.9 %all-to-all-start = ((s32[8,1,32]{2,1,0:T(1,128)}), s32[8,1,32]{2,1,0:T(1,128)S(1)}, u32[]{:S(2)}, u32[]{:S(2)}) async-start(s32[8,1,32]{2,1,0:T(1,128)} %bitcast.1), calls=%async_computation | async-start | bytes 8192 | tf_op jit(solution)/shard_map/all_to_all | solution.py:96
where the time goes:
time: 55.4 us; the launch traced here: 55.1 us
  blocking collectives  27.6 us (50%)
  starting transfers between devices  8.52 us (15%)
  local copies, waits for them, and re-layouts  7.25 us (13%)
  waiting for transfers between devices  6.04 us (11%)
  other arithmetic  3 us (5%)
  matrix products  1.86 us (3%)
  between operations  0.8 us (1%)
    psum x1, blocking collectives, local(): partial_sum = lax.psum(partial_sum, 'rep')  19.4 us
    all_gather x1, blocking collectives, local(): update = lax.all_gather(my_share, 'grp', axis=0, tiled=True)  8.26 us
    all_to_all x1, starting transfers between devices, local(): lax.all_to_all(shaped[0], 'grp', split_axis=0, concat_axis=2, tiled=True)  5.21 us
    all_to_all x1, waiting for transfers between devices, local(): lax.all_to_all(shaped[1], 'grp', split_axis=0, concat_axis=2, tiled=True)  3.79 us
    all_to_all x1, starting transfers between devices, local(): lax.all_to_all(shaped[1], 'grp', split_axis=0, concat_axis=2, tiled=True)  3.31 us
    gather x3, local copies, waits for them, and re-layouts, local(): jnp.take_along_axis(transform_coefficients, picked, axis=1)  2.56 us
    all_to_all x1, waiting for transfers between devices, local(): lax.all_to_all(shaped[0], 'grp', split_axis=0, concat_axis=2, tiled=True)  2.26 us
    unnamed x8, local copies, waits for them, and re-layouts  1.44 us
  transfers between devices with their start and end apart: 2, of which 2 were waited for; matrix products, arithmetic and copies ran while one was open for 6% of the time, Pallas kernels for 0%

commit v1 on v0

--- a/solution.py
+++ b/solution.py
@@ -96,7 +96,7 @@
             lax.all_to_all(shaped[1], "grp", split_axis=0, concat_axis=2, tiled=True),
         )
     )
-    partial_sum = lax.psum(partial_sum, "rep")
+    partial_sum = jnp.sum(lax.all_gather(partial_sum, "rep"), axis=0)
     my_share = decode(partial_sum, cosines).astype(jnp.bfloat16)
     update = lax.all_gather(my_share, "grp", axis=0, tiled=True)
     return (update, residual_momentum)

time: 55.4 us -> 49.7 us (0.90)
  blocking collectives: 27.6 us -> 21.7 us
    psum x1 -> x0, blocking collectives: 19.4 us -> none  [local(): partial_sum = lax.psum(partial_sum, 'rep')]
    all_gather x0 -> x1, blocking collectives: none -> 13.4 us  [local(): partial_sum = jnp.sum(lax.all_gather(partial_sum, 'rep'), axis=0)]
where the time goes in v1:
time: 49.7 us; the launch traced here: 49.4 us
  blocking collectives  21.7 us (44%)
  starting transfers between devices  8.52 us (17%)
  local copies, waits for them, and re-layouts  7.42 us (15%)
  waiting for transfers between devices  6.04 us (12%)
  other arithmetic  3.06 us (6%)
  matrix products  1.87 us (4%)
  between operations  0.8 us (2%)
    all_gather x1, blocking collectives, local(): partial_sum = jnp.sum(lax.all_gather(partial_sum, 'rep'), axis=0)  13.4 us
    all_gather x1, blocking collectives, local(): update = lax.all_gather(my_share, 'grp', axis=0, tiled=True)  8.26 us
    all_to_all x1, starting transfers between devices, local(): lax.all_to_all(shaped[0], 'grp', split_axis=0, concat_axis=2, tiled=True)  5.21 us
    all_to_all x1, waiting for transfers between devices, local(): lax.all_to_all(shaped[1], 'grp', split_axis=0, concat_axis=2, tiled=True)  3.79 us
    all_to_all x1, starting transfers between devices, local(): lax.all_to_all(shaped[1], 'grp', split_axis=0, concat_axis=2, tiled=True)  3.31 us
    gather x3, local copies, waits for them, and re-layouts, local(): jnp.take_along_axis(transform_coefficients, picked, axis=1)  2.56 us
    all_to_all x1, waiting for transfers between devices, local(): lax.all_to_all(shaped[0], 'grp', split_axis=0, concat_axis=2, tiled=True)  2.26 us
    unnamed x8, local copies, waits for them, and re-layouts  1.44 us
  transfers between devices with their start and end apart: 2, of which 2 were waited for; matrix products, arithmetic and copies ran while one was open for 6% of the time, Pallas kernels for 0%

profile of v1, /device:TPU:0, one launch (start us, length us, event | category | flops | bytes accessed | tf_op | source)
XLA Modules:
  0.0 49.4 jit_solution(2553000437007644842)
XLA Ops:
  0.6 0.7 %compare_and_fusion = pred[8]{0:T(512)(128)(4,1)S(1)} fusion(s32[8]{0:T(128)} %param.7), kind=kLoop, calls=%fused_computation.49 | loop fusion | flops 48 | bytes 40 | tf_op jit(solution)/shard_map/jit(_take)/and | solution.py:90
  1.4 0.6 %copy-done = s32[8,32]{1,0:T(8,128)S(1)} copy-done((s32[8,32]{1,0:T(8,128)S(1)}, s32[8,32]{1,0:T(8,128)}, u32[]{:S(2)}) %copy-start) | copy-done | bytes 1048
  2.1 0.1 cosine_multiply_fusion
  2.4 0.2 reshape.315
  2.5 0.3 convolution_bitcast_fusion.2
  2.8 0.3 convolution_bitcast_fusion.1
  3.1 0.1 copy.19
  3.2 0.2 reshape.316
  3.4 2.4 %gather_fusion.2 = bf16[256]{0:T(256)(128)(2,1)S(1)} fusion(bf16[8,4096]{1,0:T(8,128)(2,1)S(1)} %reshape.316, s32[256]{0:T(256)S(1)} %reshape.336), kind=kCustom, calls=%fused_computation.2 | custom fusion | bytes 3072 | tf_op jit(solution)/shard_map/jit(take_along_axis)/gather | solution.py:85
  5.9 0.6 %gather_fusion.1 = bf16[8,32]{1,0:T(8,128)(2,1)S(1)} fusion(bf16[8,32]{1,0:T(8,128)(2,1)S(1)} %select_convert_fusion, s32[1024]{0:T(1024)S(1)} %pad_clamp_fusion), kind=kCustom, calls=%fused_computation.1 | custom fusion | bytes 1056 | tf_op jit(solution)/shard_map/jit(_take)/gather | solution.py:90
  6.5 0.6 %copy.20 = bf16[8,1,32]{2,1,0:T(2,128)(2,1)} copy(bf16[8,1,32]{2,0,1:T(8,128)(2,1)S(1)} %bitcast_select_fusion.1) | data formatting | bytes 1024 | tf_op jit(solution)/shard_map/jit(_take)/select_n | solution.py:90
  7.1 5.2 %all-to-all-start.1 = ((bf16[8,1,32]{2,1,0:T(2,128)(2,1)}), bf16[8,1,32]{2,1,0:T(2,128)(2,1)S(1)}, u32[]{:S(2)}, u32[]{:S(2)}) async-start(bf16[8,1,32]{2,1,0:T(2,128)(2,1)} %copy.20), calls=%async_computation.1 | async-start | bytes 8192 | tf_op jit(solution)/shard_map/all_to_all | solution.py:95
  12.3 0.6 %gather_fusion = s32[8,32]{1,0:T(8,128)S(1)} fusion(s32[8,32]{1,0:T(8,128)S(1)} %copy-done, s32[1024]{0:T(1024)S(1)} %pad_clamp_fusion), kind=kCustom, calls=%fused_computation | custom fusion | bytes 2080 | tf_op jit(solution)/shard_map/jit(_take)/gather | solution.py:91
  12.9 0.6 %fusion = f32[8,64,64]{1,2,0:T(8,128)S(1)} fusion(s32[8,32]{1,0:T(8,128)S(1)} %get-tuple-element.45, s32[8,32]{1,0:T(8,128)S(1)} %get-tuple-element.44, bf16[8,32]{1,0:T(8,128)(2,1)S(1)} %select_convert_fusion, bf16[64,64]{1,0:T(8,128)(2,1)S(1)} %convert_element_type.42), kind=kOutput, calls=%fused_computation.7 | convolution fusion | flops 6373376 | bytes 141824 | tf_op jit(solution)/shard_map/cij,jb->cib/dot_general | solution.py:35
  13.5 0.3 convolution_bitcast_fusion
  13.8 0.7 %bitcast_select_fusion = s32[8,1,32]{2,0,1:T(8,128)} fusion(s32[8,32]{1,0:T(8,128)S(1)} %gather_fusion, pred[8]{0:T(512)(128)(4,1)S(1)} %compare_and_fusion), kind=kLoop, calls=%fused_computation.40 | loop fusion | flops 256 | bytes 2056 | tf_op jit(solution)/shard_map/jit(_take)/select_n | solution.py:91
  14.4 0.1 copy.23
  14.6 0.1 reshape.319
  14.7 2.3 %all-to-all-done.1 = bf16[8,1,32]{2,1,0:T(2,128)(2,1)S(1)} async-done(((bf16[8,1,32]{2,1,0:T(2,128)(2,1)}), bf16[8,1,32]{2,1,0:T(2,128)(2,1)S(1)}, u32[]{:S(2)}, u32[]{:S(2)}) %all-to-all-start.1) | async-done | bytes 544 | tf_op jit(solution)/shard_map/all_to_all | solution.py:95
  16.9 3.3 %all-to-all-start = ((s32[8,1,32]{2,1,0:T(1,128)}), s32[8,1,32]{2,1,0:T(1,128)S(1)}, u32[]{:S(2)}, u32[]{:S(2)}) async-start(s32[8,1,32]{2,1,0:T(1,128)} %bitcast.1), calls=%async_computation | async-start | bytes 8192 | tf_op jit(solution)/shard_map/all_to_all | solution.py:96
  20.3 0.6 %subtract_convert_fusion = bf16[8,4096]{1,0:T(8,128)(2,1)} fusion(f32[8,4096]{1,0:T(8,128)S(1)} %reshape.319, bf16[8,4096]{1,0:T(8,128)(2,1)S(1)} %copy-done.1), kind=kLoop, calls=%fused_computation.10 | loop fusion | flops 98304 | bytes 262144 | tf_op jit(solution)/shard_map/convert_element_type | solution.py:89
  21.0 3.8 %all-to-all-done = s32[8,1,32]{2,1,0:T(1,128)S(1)} async-done(((s32[8,1,32]{2,1,0:T(1,128)}), s32[8,1,32]{2,1,0:T(1,128)S(1)}, u32[]{:S(2)}, u32[]{:S(2)}) %all-to-all-start) | async-done | bytes 1056 | tf_op jit(solution)/shard_map/all_to_all | solution.py:96
  24.8 0.5 %broadcast.298 = s32[]{:T(128)} broadcast(s32[]{:T(128)} %constant.140.clone.1), dimensions={} | broadcast | bytes 8 | tf_op jit(solution)/shard_map/all_to_all | solution.py:96
  25.3 0.7 %reduce.7 = s32[8,32]{1,0:T(8,128)S(1)} reduce(s32[8,1,32]{2,1,0:T(1,128)S(1)} %all-to-all-done, s32[]{:T(128)} %broadcast.298), dimensions={1}, to_apply=%all_to_all.4.reduce_sub_computation.3 | reduce | bytes 2052 | tf_op jit(solution)/shard_map/all_to_all | solution.py:96
  26.1 0.1 fusion.10
  26.2 0.1 broadcast_in_dim.108
  26.3 13.4 %all_gather.6 = f32[4,1,4096]{2,1,0:T(1,128)S(1)} all-gather(f32[1,1,4096]{2,1,0:T(1,128)S(1)} %broadcast_in_dim.108), channel_id=1, replica_groups=mesh['grp'=8,'rep'=4] {'rep'}, dimensions={0}, use_global_device_ids=true | all-gather | bytes 81920 | tf_op jit(solution)/shard_map/all_gather | solution.py:99
  39.9 0.1 fusion.29
  40.0 0.2 fusion.1
  40.3 0.1 copy.21
  40.4 8.3 %all-gather = bf16[8,1,4096]{2,1,0:T(2,128)(2,1)S(1)} all-gather(bf16[1,1,4096]{2,1,0:T(2,128)(2,1)S(1)} %reshape.349), channel_id=1, replica_groups=mesh['grp'=8,'rep'=4] {'grp'}, dimensions={0}, use_global_device_ids=true | all-gather | bytes 73728 | tf_op jit(solution)/shard_map/all_gather | solution.py:101
  48.7 0.7 %copy.27 = bf16[8,1,4096]{2,0,1:T(8,128)(2,1)} copy(bf16[8,1,4096]{2,1,0:T(2,128)(2,1)S(1)} %all-gather) | data formatting | bytes 131072
  (24 shorter events, 0.8 us)
Async XLA Ops:
  0.6 0.7 %copy-start.2 = (s32[8]{0:T(128)S(1)}, s32[8]{0:T(128)}, u32[]{:S(2)}) copy-start(s32[8]{0:T(128)} %param.7) | copy-start | bytes 100
  1.4 0.7 %copy-start = (s32[8,32]{1,0:T(8,128)S(1)}, s32[8,32]{1,0:T(8,128)}, u32[]{:S(2)}) copy-start(s32[8,32]{1,0:T(8,128)} %param.6) | copy-start | bytes 3076
  1.4 1.0 %copy-start.1 = (bf16[8,4096]{1,0:T(8,128)(2,1)S(1)}, bf16[8,4096]{1,0:T(8,128)(2,1)}, u32[]{:S(2)}) copy-start(bf16[8,4096]{1,0:T(8,128)(2,1)} %param.5) | copy-start | bytes 196612
  7.1 9.8 %all-to-all-start.1 = ((bf16[8,1,32]{2,1,0:T(2,128)(2,1)}), bf16[8,1,32]{2,1,0:T(2,128)(2,1)S(1)}, u32[]{:S(2)}, u32[]{:S(2)}) async-start(bf16[8,1,32]{2,1,0:T(2,128)(2,1)} %copy.20), calls=%async_computation.1 | async-start | bytes 8192 | tf_op jit(solution)/shard_map/all_to_all | solution.py:95
  16.9 7.9 %all-to-all-start = ((s32[8,1,32]{2,1,0:T(1,128)}), s32[8,1,32]{2,1,0:T(1,128)S(1)}, u32[]{:S(2)}, u32[]{:S(2)}) async-start(s32[8,1,32]{2,1,0:T(1,128)} %bitcast.1), calls=%async_computation | async-start | bytes 8192 | tf_op jit(solution)/shard_map/all_to_all | solution.py:96
